TPU v7x, 32 devices: a whole 2x2x4 slice. The times are simulated.
32 devices in a mesh: dp: 8 (over z, y), expert: 4 (over x, core).
Axes of the slice: x: 2, y: 2, z: 4, core: 2. Of those that a mesh axis runs over, the one named last changes fastest.
Arguments:
- queries: bfloat16 [4096, 4096], P('dp', 'expert'), may hold values from -6 to 6
- key_states: bfloat16 [4096, 4096], P('dp', 'expert'), may hold values from -6 to 6
- value_states: bfloat16 [4096, 4096], P('dp', 'expert'), may hold values from -6 to 6
- doc_lengths: int32 [8, 8], replicated, may hold values from 0 to 512, as said below
- move_plan: int32 [8, 2], replicated, may hold values from 0 to 7, as said below
- expert_ids: int32 [4096, 8], P('dp'), may hold values from 0 to 15, all different within a row; in each aligned block of 512 rows (0 to 511, 512 to 1023, ...) at most 384 rows name the same one
- gate_weights: float32 [4096, 8], P('dp'), may hold values from 0.05 to 0.5
- expert_weight: bfloat16 [16, 4096, 1024], P('expert'), may hold values from -0.29882812 to 0.29882812
Outputs:
- attended: bfloat16 [4096, 4096], P('dp', 'expert')
- combined: bfloat16 [4096, 1024], P('dp', 'expert')
- row_load: float32 [8], P('dp')
Inputs may be any that keep to these rules, and one draw needn't show every extreme that they name: `doc_lengths`: each row's entries are the lengths of its packed documents in order and sum to 512; a zero marks an absent document; some row holds a single document. move_plan[r, 0] is r itself or the row half the dp axis away, (r + 8 / 2) mod 8; a row is handed to its partner only if its pairs in all exceed the partner's, so two partners never both move; move_plan[r, 1] is a block number below 2; at least one row moves a block. `expert_ids`: each token names 8 different experts; among the 512 tokens of one row no expert is named by more than 384 tokens.
All inputs are finite; a program needn't handle non-finite values.
Results may differ from a plain program's by a relative error of at most 0.0095.
Values may be sent and summed in bfloat16 or wider, within the bound.
A program may use at most 128 MiB of HBM per device.

v0:
```python
import jax
import jax.numpy as jnp
from jax import lax
from jax.sharding import PartitionSpec as P

HEAD_DIM = 128
QBLOCK = 128
BLOCKS = 4
EXPERTS = 16
CAP = 384


def token_starts(row_lengths, row_count):
    bounds = jnp.cumsum(row_lengths)
    positions = jnp.arange(row_count, dtype=jnp.int32)
    return jnp.max(jnp.where(bounds[None, :] <= positions[:, None], bounds[None, :], 0), axis=1)


def block_pairs(row_lengths, row_count):
    positions = jnp.arange(row_count, dtype=jnp.int32)
    reach = positions - token_starts(row_lengths, row_count) + 1
    return reach.reshape(BLOCKS, QBLOCK).sum(axis=1)


def attend(query_rows, key_rows, value_rows, query_positions, query_starts):
    query_count = query_rows.shape[0]
    key_count = key_rows.shape[0]
    head_count = query_rows.shape[1] // HEAD_DIM
    query_heads = query_rows.reshape(query_count, head_count, HEAD_DIM)
    key_heads = key_rows.reshape(key_count, head_count, HEAD_DIM)
    value_heads = value_rows.reshape(key_count, head_count, HEAD_DIM)
    scores = jnp.einsum(
        "qhd,khd->hqk", query_heads, key_heads, preferred_element_type=jnp.float32
    ) * HEAD_DIM ** (-0.5)
    key_positions = jnp.arange(key_count, dtype=jnp.int32)
    allowed = (key_positions[None, :] <= query_positions[:, None]) & (
        key_positions[None, :] >= query_starts[:, None]
    )
    scores = jnp.where(allowed[None], scores, -jnp.inf)
    weights = jax.nn.softmax(scores, axis=-1).astype(jnp.bfloat16)
    output = jnp.einsum("hqk,khd->qhd", weights, value_heads, preferred_element_type=jnp.float32)
    return output.reshape(query_count, head_count * HEAD_DIM).astype(jnp.bfloat16)


def shards(
    queries,
    key_states,
    value_states,
    doc_lengths,
    move_plan,
    expert_ids,
    gate_weights,
    expert_weight,
):
    dp_size = lax.axis_size("dp")
    group_size = lax.axis_size("expert")
    own_row = lax.axis_index("dp")
    partner = (own_row + dp_size // 2) % dp_size
    row_count = queries.shape[0]
    positions = jnp.arange(row_count, dtype=jnp.int32)
    own_lengths = lax.dynamic_index_in_dim(doc_lengths, own_row, 0, keepdims=False)
    partner_lengths = lax.dynamic_index_in_dim(doc_lengths, partner, 0, keepdims=False)
    own_starts = token_starts(own_lengths, row_count)
    own_plan = lax.dynamic_index_in_dim(move_plan, own_row, 0, keepdims=False)
    partner_plan = lax.dynamic_index_in_dim(move_plan, partner, 0, keepdims=False)
    moving = own_plan[0] != own_row
    incoming = partner_plan[0] != partner
    own_block = own_plan[1]
    their_block = partner_plan[1]

    def run_block(block_index):
        low_row = block_index * QBLOCK
        high_row = low_row + QBLOCK
        return attend(
            queries[low_row:high_row],
            key_states[:high_row],
            value_states[:high_row],
            positions[low_row:high_row],
            own_starts[low_row:high_row],
        )

    attended = jnp.concatenate([run_block(block_index) for block_index in range(BLOCKS)], 0)
    own_pairs = block_pairs(own_lengths, row_count)
    partner_pairs = block_pairs(partner_lengths, row_count)
    row_work = (
        jnp.sum(own_pairs)
        - jnp.where(moving, own_pairs[own_block], 0)
        + jnp.where(incoming, partner_pairs[their_block], 0)
    )
    row_load = (row_work.astype(jnp.float32) / (QBLOCK * QBLOCK)).reshape(1)
    local_experts = EXPERTS // group_size
    expert_range = jnp.arange(EXPERTS, dtype=jnp.int32)
    matches = expert_ids[:, :, None] == expert_range[None, None, :]
    member = jnp.any(matches, axis=1)
    gate_table = jnp.sum(jnp.where(matches, gate_weights[:, :, None], 0.0), axis=1)
    earlier = (positions[None, :] < positions[:, None]).astype(jnp.bfloat16)
    slot_counts = jnp.dot(earlier, member.astype(jnp.bfloat16), preferred_element_type=jnp.float32)
    slot_of = slot_counts.astype(jnp.int32)
    slot_range = jnp.arange(CAP, dtype=jnp.int32)
    dispatch_hot = member.T[:, None, :] & (slot_of.T[:, None, :] == slot_range[None, :, None])
    filled = jnp.any(dispatch_hot, axis=2)
    source = jnp.sum(jnp.where(dispatch_hot, positions[None, None, :], 0), axis=2) + jnp.where(
        filled, 0, row_count
    )
    source = source.reshape(-1)
    member_index = lax.axis_index("expert")
    chosen_rows = lax.dynamic_slice_in_dim(
        source, member_index * local_experts * CAP, local_experts * CAP, 0
    )
    piece = lax.all_gather(attended, "expert", axis=1, tiled=True)
    extended = jnp.concatenate([piece, jnp.zeros((1, piece.shape[1]), piece.dtype)], 0)
    picked = extended[chosen_rows].reshape(local_experts, CAP, piece.shape[1])
    summed = jnp.einsum("ecf,efg->ecg", picked, expert_weight, preferred_element_type=jnp.float32)
    activated = jax.nn.silu(summed).astype(jnp.bfloat16)[None]
    spread = lax.all_to_all(activated, "expert", split_axis=3, concat_axis=0, tiled=True)
    outputs_table = spread.reshape(EXPERTS, CAP, spread.shape[3])
    selected = jnp.einsum(
        "ect,ecg->teg",
        dispatch_hot.astype(jnp.bfloat16),
        outputs_table,
        preferred_element_type=jnp.float32,
    )
    combined = jnp.sum(selected * gate_table[:, :, None], axis=1).astype(jnp.bfloat16)
    return (attended, combined, row_load)


def solution(mesh):
    in_specs = (
        P("dp", "expert"),
        P("dp", "expert"),
        P("dp", "expert"),
        P(),
        P(),
        P("dp", None),
        P("dp", None),
        P("expert", None, None),
    )
    out_specs = (P("dp", "expert"), P("dp", "expert"), P("dp"))
    return jax.shard_map(shards, mesh=mesh, in_specs=in_specs, out_specs=out_specs, check_vma=False)
```

profile of v0, /device:TPU:0, one launch (start us, length us, event | category | flops | bytes accessed | tf_op | source)
XLA Modules:
  0.0 178.1 jit_solution(11677466727423004778)
XLA Ops:
  7.2 0.8 fusion.53
  8.0 0.2 reduce-window.16
  8.3 1.3 fusion.57
  9.6 0.2 copy.120
  9.8 0.4 copy.121
  10.3 1.6 multiply_select_fusion.2
  11.8 0.8 fusion.64
  12.6 0.2 copy.118
  12.8 0.2 copy.119
  13.1 0.3 fusion.19
  13.5 0.6 fusion.65
  14.1 0.6 copy-done
  14.7 1.3 copy.115
  16.0 1.2 copy.95
  17.2 4.2 %convolution_convert_fusion.2 = bf16[8,128,128]{1,2,0:T(8,128)(2,1)S(1)} fusion(bf16[384,8,128]{0,2,1:T(8,128)(2,1)} %bitcast.113, f32[8,128]{1,0:T(8,128)S(1)} %fusion.64, f32[8,128,384]{2,1,0:T(8,128)} %multiply_select_fusion.2), kind=kOutput, calls=%fused_computation.34 | convolution fusion | flops 101975424 | bytes 2625536 | tf_op jit(solution)/shard_map/hqk,khd->qhd/dot_general | solution.py:41
  21.4 0.9 copy.102
  22.2 0.2 copy.90
  22.5 1.9 %convolution_convert_fusion.3 = bf16[8,128,128]{1,2,0:T(8,128)(2,1)S(1)} fusion(bf16[256,8,128]{0,2,1:T(8,128)(2,1)S(1)} %bitcast.114, f32[8,128]{1,0:T(8,128)S(1)} %fusion.65, f32[8,128,256]{2,1,0:T(8,128)S(1)} %fusion.19), kind=kOutput, calls=%fused_computation.35 | convolution fusion | flops 68027648 | bytes 1839104 | tf_op jit(solution)/shard_map/hqk,khd->qhd/dot_general | solution.py:41
  24.4 0.2 copy.101
  24.6 0.2 copy.116
  24.8 0.2 copy.117
  25.0 0.3 fusion.22
  25.4 0.2 copy.84
  25.6 0.3 convolution_convert_fusion.1
  25.9 0.1 copy.100
  26.1 0.2 copy.122
  26.4 2.3 %fusion.61 = (f32[8,128]{1,0:T(8,128)S(1)}, f32[8,128,512]{2,1,0:T(8,128)}) fusion(pred[128,512]{1,0:T(8,128)(4,1)S(1)} %fusion.32, bf16[128,8,128]{0,2,1:T(8,128)(2,1)S(1)} %bitcast.115, bf16[512,1024]{1,0:T(8,128)(2,1)S(1)} %copy-done.1), kind=kOutput, calls=%fused_computation.98 | convolution fusion | flops 136315392 | bytes 3477504 | tf_op jit(solution)/shard_map/sub | solution.py:40
  28.7 2.2 %convolution_convert_fusion = bf16[8,128,128]{1,2,0:T(8,128)(2,1)S(1)} fusion(bf16[512,8,128]{0,2,1:T(8,128)(2,1)S(1)} %bitcast.108, f32[8,128,512]{2,1,0:T(8,128)} %get-tuple-element.26, f32[8,128]{1,0:T(8,128)S(1)} %get-tuple-element.25), kind=kOutput, calls=%fused_computation.32 | convolution fusion | flops 135397376 | bytes 3411968 | tf_op jit(solution)/shard_map/hqk,khd->qhd/dot_general | solution.py:41
  30.9 0.1 copy.103
  31.1 1.0 pad_maximum_fusion
  32.2 0.2 convolution_convert_fusion.4
  32.4 2.1 %fusion.7 = pred[16,384]{1,0:T(8,128)(4,1)S(1)} fusion(s32[16,512]{1,0:T(8,128)S(1)} %convolution_convert_fusion.4, pred[16,512]{1,0:T(8,128)(4,1)S(1)} %bitcast.121), kind=kLoop, calls=%fused_computation.9 | loop fusion | flops 9431040 | bytes 47104 | tf_op jit(solution)/shard_map/reduce_or | solution.py:101
  34.5 2.8 %select_reduce_fusion = s32[16,384]{1,0:T(8,128)S(1)} fusion(s32[16,512]{1,0:T(8,128)S(1)} %convolution_convert_fusion.4, pred[16,512]{1,0:T(8,128)(4,1)S(1)} %bitcast.122), kind=kLoop, calls=%fused_computation.5 | loop fusion | flops 12576768 | bytes 65536 | tf_op jit(solution)/shard_map/reduce_sum | solution.py:102
  37.4 32.1 %all-gather.2.cloned.1.call-done = bf16[512,4096]{1,0:T(8,128)(2,1)} async-done(((bf16[512,1024]{1,0:T(8,128)(2,1)}), bf16[512,4096]{1,0:T(8,128)(2,1)}) %all-gather.2.cloned.1.call-update) | async-done | bytes 4194320 | tf_op jit(solution)/shard_map/all_gather | solution.py:110
  69.5 4.7 %concatenate.7 = bf16[513,4096]{1,0:T(8,128)(2,1)} pad(bf16[512,4096]{1,0:T(8,128)(2,1)} %all-gather.2.cloned.1.call-done, bf16[]{:T(256)} %constant.66.clone.1), padding=0_1x0_0 | pad | bytes 8396802 | tf_op jit(solution)/shard_map/concatenate | solution.py:111
  74.2 25.0 %gather_fusion = bf16[1536,4096]{1,0:T(8,128)(2,1)} fusion(bf16[513,4096]{1,0:T(8,128)(2,1)} %concatenate.7, s32[2048]{0:T(1024)S(1)} %pad_clamp_fusion), kind=kCustom, calls=%fused_computation | custom fusion | bytes 25171968 | tf_op jit(solution)/shard_map/gather | solution.py:112
  99.2 21.3 %fusion.11 = bf16[1,4,384,1024]{3,2,1,0:T(8,128)(2,1)S(1)} fusion(bf16[4,384,4096]{2,1,0:T(8,128)(2,1)} %bitcast.99, bf16[4,4096,1024]{2,1,0:T(8,128)(2,1)} %param.15), kind=kOutput, calls=%fused_computation.15 | convolution fusion | flops 12892766208 | bytes 49283072 | tf_op jit(solution)/shard_map/ecf,efg->ecg/dot_general | solution.py:113
  120.5 3.8 %copy.104 = bf16[1,4,384,1024]{2,1,0,3:T(4,128)(2,1)} copy(bf16[1,4,384,1024]{3,2,1,0:T(8,128)(2,1)S(1)} %fusion.11) | data formatting | bytes 6291456 | tf_op jit(solution)/shard_map/broadcast_in_dim | solution.py:114
  124.3 4.1 %all-to-all-start = ((bf16[1,4,384,1024]{2,1,0,3:T(4,128)(2,1)}), bf16[1,4,384,1024]{2,1,0,3:T(4,128)(2,1)S(1)}, u32[]{:S(2)}, u32[]{:S(2)}) async-start(bf16[1,4,384,1024]{2,1,0,3:T(4,128)(2,1)} %copy.104), calls=%async_computation | async-start | bytes 6291456 | tf_op jit(solution)/shard_map/all_to_all | solution.py:115
  128.5 0.5 fusion.59
  132.1 0.2 reduce-window.17
  133.7 0.6 dynamic_slice.26
  134.9 0.6 add_reduce_fusion
  137.0 0.6 dynamic_slice.29
  138.3 26.6 %all-to-all-done = bf16[1,4,384,1024]{2,1,0,3:T(4,128)(2,1)S(1)} async-done(((bf16[1,4,384,1024]{2,1,0,3:T(4,128)(2,1)}), bf16[1,4,384,1024]{2,1,0,3:T(4,128)(2,1)S(1)}, u32[]{:S(2)}, u32[]{:S(2)}) %all-to-all-start) | async-done | bytes 3145760 | tf_op jit(solution)/shard_map/all_to_all | solution.py:115
  165.0 0.6 copy.105
  165.5 3.8 %fusion.8 = bf16[512,256]{0,1:T(8,128)(2,1)S(1)} fusion(f32[512,16]{0,1:T(8,128)S(1)} %select_reduce_fusion.1, bf16[16,384,256]{1,2,0:T(8,128)(2,1)S(1)} %bitcast.101, s32[16,512]{1,0:T(8,128)S(1)} %convolution_convert_fusion.4, pred[16,512]{1,0:T(8,128)(4,1)S(1)} %bitcast.123), kind=kOutput, calls=%fused_computation.11 | convolution fusion | flops 1620967424 | bytes 3481600 | tf_op jit(solution)/shard_map/ect,ecg->teg/dot_general | solution.py:117
  169.3 0.8 copy.106
  (52 shorter events, 1.3 us)
Async XLA Ops:
  7.2 2.6 %slice-start.3 = ((bf16[512,1024]{1,0:T(8,128)(2,1)}), bf16[384,1024]{1,0:T(8,128)(2,1)S(1)}, s32[]{:S(2)}) async-start(bf16[512,1024]{1,0:T(8,128)(2,1)} %param.9), calls=%async_computation.5 | async-start | bytes 1572864 | tf_op jit(solution)/shard_map/slice | solution.py:76
  7.2 62.3 %all-gather.2.cloned.1.call-start = ((), (), s32[]{:S(2)}) async-start(), calls=%async_computation.1 | async-start | bytes 5242880 | tf_op jit(solution)/shard_map/all_gather | solution.py:110
  10.2 2.5 %slice-start.4 = ((bf16[512,1024]{1,0:T(8,128)(2,1)}), bf16[256,1024]{1,0:T(8,128)(2,1)S(1)}, s32[]{:S(2)}) async-start(bf16[512,1024]{1,0:T(8,128)(2,1)} %param.9), calls=%async_computation.6 | async-start | bytes 1048576 | tf_op jit(solution)/shard_map/slice | solution.py:76
  13.5 1.2 copy-start
  14.1 1.9 %slice-start = ((bf16[512,1024]{1,0:T(8,128)(2,1)}), bf16[384,1024]{1,0:T(8,128)(2,1)S(1)}, s32[]{:S(2)}) async-start(bf16[512,1024]{1,0:T(8,128)(2,1)} %param.10), calls=%async_computation.2 | async-start | bytes 1572864 | tf_op jit(solution)/shard_map/slice | solution.py:77
  17.2 5.0 %slice-start.1 = ((bf16[512,1024]{1,0:T(8,128)(2,1)}), bf16[256,1024]{1,0:T(8,128)(2,1)S(1)}, s32[]{:S(2)}) async-start(bf16[512,1024]{1,0:T(8,128)(2,1)} %param.10), calls=%async_computation.3 | async-start | bytes 1048576 | tf_op jit(solution)/shard_map/slice | solution.py:77
  22.4 2.3 %slice-start.5 = ((bf16[512,1024]{1,0:T(8,128)(2,1)}), bf16[128,1024]{1,0:T(8,128)(2,1)S(1)}, s32[]{:S(2)}) async-start(bf16[512,1024]{1,0:T(8,128)(2,1)} %param.9), calls=%async_computation.7 | async-start | bytes 524288 | tf_op jit(solution)/shard_map/slice | solution.py:76
  22.4 3.0 %slice-start.2 = ((bf16[512,1024]{1,0:T(8,128)(2,1)}), bf16[128,1024]{1,0:T(8,128)(2,1)S(1)}, s32[]{:S(2)}) async-start(bf16[512,1024]{1,0:T(8,128)(2,1)} %param.10), calls=%async_computation.4 | async-start | bytes 524288 | tf_op jit(solution)/shard_map/slice | solution.py:77
  24.8 1.6 copy-start.1
  25.9 2.8 %copy-start.2 = (bf16[512,1024]{0,1:T(8,128)(2,1)S(1)}, bf16[512,1024]{0,1:T(8,128)(2,1)}, u32[]{:S(2)}) copy-start(bf16[512,1024]{0,1:T(8,128)(2,1)} %copy.115) | copy-start | bytes 3145732
  28.7 2.3 %copy-start.3 = (bf16[128,1024]{1,0:T(8,128)(2,1)S(1)}, bf16[128,1024]{1,0:T(8,128)(2,1)}, u32[]{:S(2)}) copy-start(bf16[128,1024]{1,0:T(8,128)(2,1)} %copy.102) | copy-start | bytes 786436
  30.9 1.2 copy-start.4
  124.3 4.1 %copy-start.6 = (s32[8,2]{0,1:T(2,128)S(1)}, s32[8,2]{0,1:T(2,128)}, u32[]{:S(2)}) copy-start(s32[8,2]{0,1:T(2,128)} %param.12) | copy-start | bytes 196
  124.3 14.0 %copy-start.5 = (f32[512,8]{0,1:T(8,128)S(1)}, f32[512,8]{0,1:T(8,128)}, u32[]{:S(2)}) copy-start(f32[512,8]{0,1:T(8,128)} %param.14) | copy-start | bytes 49156
  124.3 40.7 %all-to-all-start = ((bf16[1,4,384,1024]{2,1,0,3:T(4,128)(2,1)}), bf16[1,4,384,1024]{2,1,0,3:T(4,128)(2,1)S(1)}, u32[]{:S(2)}, u32[]{:S(2)}) async-start(bf16[1,4,384,1024]{2,1,0,3:T(4,128)(2,1)} %copy.104), calls=%async_computation | async-start | bytes 6291456 | tf_op jit(solution)/shard_map/all_to_all | solution.py:115
Sparse Core Ops, SparseCore 0:
  32.2 37.1 all-gather.1
where the time goes:
time: 179 us; the launch traced here: 178 us
  waiting for transfers between devices  58.7 us (33%)
  local copies, waits for them, and re-layouts  44.9 us (25%)
  matrix products  39.8 us (22%)
  between operations  22.6 us (13%)
  other arithmetic  7.99 us (4%)
  starting transfers between devices  4.13 us (2%)
    all_gather x1, waiting for transfers between devices, shards(): piece = lax.all_gather(attended, 'expert', axis=1, tiled=True)  32.1 us
    all_to_all x1, waiting for transfers between devices, shards(): lax.all_to_all(activated, 'expert', split_axis=3, concat_axis=0, tiled=True)  26.6 us
    gather x1, local copies, waits for them, and re-layouts, shards(): picked = extended[chosen_rows].reshape(local_experts, CAP, piece.shape[1])  25 us
    dot_general x1, matrix products, shards(): jnp.einsum('ecf,efg->ecg', picked, expert_weight, preferred_element_type=...  21.3 us
    dot_general x4, matrix products, attend(): jnp.einsum('hqk,khd->qhd', weights, value_heads, preferred_element_type=j...  8.57 us
    concatenate x1, local copies, waits for them, and re-layouts, shards(): jnp.concatenate([piece, jnp.zeros((1, piece.shape[1]), piece.dtype)], 0)  4.7 us
    all_to_all x1, starting transfers between devices, shards(): lax.all_to_all(activated, 'expert', split_axis=3, concat_axis=0, tiled=True)  4.09 us
    broadcast_in_dim x1, local copies, waits for them, and re-layouts, shards(): activated = jax.nn.silu(summed).astype(jnp.bfloat16)[None]  3.76 us
  transfers between devices with their start and end apart: 2, of which 2 were waited for; matrix products, arithmetic and copies ran while one was open for 5% of the time, Pallas kernels for 0%

commit v1 on v0

--- a/solution.py
+++ b/solution.py
@@ -107,7 +107,14 @@
     chosen_rows = lax.dynamic_slice_in_dim(
         source, member_index * local_experts * CAP, local_experts * CAP, 0
     )
-    piece = lax.all_gather(attended, "expert", axis=1, tiled=True)
+    ring = [attended]
+    for hop in range(3):
+        ring.append(lax.ppermute(ring[-1], "expert", [(dev, (dev + 1) % 4) for dev in range(4)]))
+    piece = jnp.roll(
+        jnp.concatenate(ring[::-1], axis=1),
+        (lax.axis_index("expert") + 1) * ring[0].shape[1],
+        axis=1,
+    )
     extended = jnp.concatenate([piece, jnp.zeros((1, piece.shape[1]), piece.dtype)], 0)
     picked = extended[chosen_rows].reshape(local_experts, CAP, piece.shape[1])
     summed = jnp.einsum("ecf,efg->ecg", picked, expert_weight, preferred_element_type=jnp.float32)

time: 179 us -> 172 us (0.961)
  between operations: 22.6 us -> 9.37 us
  waiting for transfers between devices: 58.7 us -> 63.8 us
    ppermute x0 -> x3, waiting for transfers between devices: none -> 37.1 us  [shards(): lax.ppermute(ring[-1], 'expert', [(dev, (dev + 1) % 4) for dev in range(4)])]
    all_gather x1 -> x0, waiting for transfers between devices: 32.1 us -> none  [shards(): piece = lax.all_gather(attended, 'expert', axis=1, tiled=True)]
    concatenate x1, local copies, waits for them, and re-layouts: 4.7 us -> 2.46 us  [shards(): jnp.concatenate([piece, jnp.zeros((1, piece.shape[1]), piece.dtype)], 0)]
    unnamed x22 -> x42, local copies, waits for them, and re-layouts: 2.83 us -> 4.49 us
  transfers between devices with their start and end apart: 2 -> 4, of which waited for: 2 -> 4; matrix products, arithmetic and copies ran while one was open for 5% -> 5% of each run, Pallas kernels for 0% -> 0%
where the time goes in v1:
time: 172 us; the launch traced here: 171 us
  waiting for transfers between devices  63.8 us (37%)
  local copies, waits for them, and re-layouts  45.7 us (27%)
  matrix products  40.5 us (24%)
  between operations  9.37 us (5%)
  other arithmetic  7.13 us (4%)
  starting transfers between devices  4.64 us (3%)
    ppermute x3, waiting for transfers between devices, shards(): lax.ppermute(ring[-1], 'expert', [(dev, (dev + 1) % 4) for dev in range(4)])  37.1 us
    all_to_all x1, waiting for transfers between devices, shards(): lax.all_to_all(activated, 'expert', split_axis=3, concat_axis=0, tiled=True)  26.6 us
    gather x1, local copies, waits for them, and re-layouts, shards(): picked = extended[chosen_rows].reshape(local_experts, CAP, piece.shape[1])  25 us
    dot_general x1, matrix products, shards(): jnp.einsum('ecf,efg->ecg', picked, expert_weight, preferred_element_type=...  21.3 us
    dot_general x4, matrix products, attend(): jnp.einsum('hqk,khd->qhd', weights, value_heads, preferred_element_type=j...  9.25 us
    unnamed x42, local copies, waits for them, and re-layouts  4.49 us
    all_to_all x1, starting transfers between devices, shards(): lax.all_to_all(activated, 'expert', split_axis=3, concat_axis=0, tiled=True)  4.09 us
    broadcast_in_dim x1, local copies, waits for them, and re-layouts, shards(): activated = jax.nn.silu(summed).astype(jnp.bfloat16)[None]  3.76 us
  transfers between devices with their start and end apart: 4, of which 4 were waited for; matrix products, arithmetic and copies ran while one was open for 5% of the time, Pallas kernels for 0%

profile of v1, /device:TPU:0, one launch (start us, length us, event | category | flops | bytes accessed | tf_op | source)
XLA Modules:
  0.0 171.1 jit_solution(16947013611806287427)
XLA Ops:
  0.7 0.8 fusion.53
  1.4 0.2 reduce-window.16
  1.7 2.0 %fusion.57 = (bf16[128,1024]{1,0:T(8,128)(2,1)}, bf16[128,1024]{1,0:T(8,128)(2,1)S(1)}, bf16[128,1024]{1,0:T(8,128)(2,1)S(1)}, bf16[128,1024]{1,0:T(8,128)(2,1)S(1)}) fusion(bf16[512,1024]{1,0:T(8,128)(2,1)} %param.8), kind=kLoop, calls=%fused_computation.103 | loop fusion | bytes 2097152 | tf_op jit(solution)/shard_map/slice | solution.py:75
  3.9 0.4 copy.121
  4.4 1.6 multiply_select_fusion.2
  6.0 0.8 fusion.64
  6.8 0.2 copy.118
  7.0 0.2 copy.119
  7.3 0.3 fusion.19
  7.6 0.6 fusion.65
  8.3 0.6 copy-done
  8.9 1.3 copy.115
  10.2 1.2 copy.95
  11.3 4.2 %convolution_convert_fusion.2 = bf16[8,128,128]{1,2,0:T(8,128)(2,1)S(1)} fusion(bf16[384,8,128]{0,2,1:T(8,128)(2,1)} %bitcast.113, f32[8,128]{1,0:T(8,128)S(1)} %fusion.64, f32[8,128,384]{2,1,0:T(8,128)} %multiply_select_fusion.2), kind=kOutput, calls=%fused_computation.34 | convolution fusion | flops 101975424 | bytes 2625536 | tf_op jit(solution)/shard_map/hqk,khd->qhd/dot_general | solution.py:41
  15.7 0.2 copy.90
  15.9 1.9 %convolution_convert_fusion.3 = bf16[8,128,128]{1,2,0:T(8,128)(2,1)S(1)} fusion(bf16[256,8,128]{0,2,1:T(8,128)(2,1)S(1)} %bitcast.114, f32[8,128]{1,0:T(8,128)S(1)} %fusion.65, f32[8,128,256]{2,1,0:T(8,128)S(1)} %fusion.19), kind=kOutput, calls=%fused_computation.35 | convolution fusion | flops 68027648 | bytes 1839104 | tf_op jit(solution)/shard_map/hqk,khd->qhd/dot_general | solution.py:41
  18.1 0.2 copy.116
  18.3 0.2 copy.117
  18.5 0.3 fusion.22
  18.9 0.2 copy.84
  19.1 1.0 convolution_convert_fusion.1
  20.1 1.2 copy.100
  21.6 2.3 %fusion.61 = (f32[8,128]{1,0:T(8,128)S(1)}, f32[8,128,512]{2,1,0:T(8,128)}) fusion(pred[128,512]{1,0:T(8,128)(4,1)S(1)} %fusion.32, bf16[128,8,128]{0,2,1:T(8,128)(2,1)S(1)} %bitcast.115, bf16[512,1024]{1,0:T(8,128)(2,1)S(1)} %copy-done.7), kind=kOutput, calls=%fused_computation.107 | convolution fusion | flops 136315392 | bytes 3477504 | tf_op jit(solution)/shard_map/sub | solution.py:40
  23.9 2.1 %convolution_convert_fusion = bf16[8,128,128]{1,2,0:T(8,128)(2,1)S(1)} fusion(bf16[512,8,128]{0,2,1:T(8,128)(2,1)S(1)} %bitcast.108, f32[8,128,512]{2,1,0:T(8,128)} %get-tuple-element.26, f32[8,128]{1,0:T(8,128)S(1)} %get-tuple-element.25), kind=kOutput, calls=%fused_computation.32 | convolution fusion | flops 135397376 | bytes 3411968 | tf_op jit(solution)/shard_map/hqk,khd->qhd/dot_general | solution.py:41
  26.3 0.7 copy-done.5
  27.0 0.5 collective-permute-start
  27.6 0.4 copy-done.8
  28.0 14.0 %collective-permute-done = bf16[512,1024]{1,0:T(8,128)(2,1)S(1)} collective-permute-done((bf16[512,1024]{1,0:T(8,128)(2,1)S(1)}, bf16[512,1024]{1,0:T(8,128)(2,1)S(1)}, u32[]{:S(2)}, u32[]{:S(2)}) %collective-permute-start) | collective-permute-done | bytes 1048608 | tf_op jit(solution)/shard_map/ppermute | solution.py:112
  42.0 0.2 convolution_convert_fusion.4
  42.3 14.0 %collective-permute-done.1 = bf16[512,1024]{1,0:T(8,128)(2,1)S(1)} collective-permute-done((bf16[512,1024]{1,0:T(8,128)(2,1)S(1)}, bf16[512,1024]{1,0:T(8,128)(2,1)S(1)}, u32[]{:S(2)}, u32[]{:S(2)}) %collective-permute-start.1) | collective-permute-done | bytes 1048608 | tf_op jit(solution)/shard_map/ppermute | solution.py:112
  56.2 2.0 %fusion.7 = pred[16,384]{1,0:T(8,128)(4,1)S(1)} fusion(s32[16,512]{1,0:T(8,128)S(1)} %convolution_convert_fusion.4, pred[16,512]{1,0:T(8,128)(4,1)S(1)} %bitcast.121), kind=kLoop, calls=%fused_computation.9 | loop fusion | flops 9431040 | bytes 47104 | tf_op jit(solution)/shard_map/reduce_or | solution.py:101
  58.3 2.8 %select_reduce_fusion = s32[16,384]{1,0:T(8,128)S(1)} fusion(s32[16,512]{1,0:T(8,128)S(1)} %convolution_convert_fusion.4, pred[16,512]{1,0:T(8,128)(4,1)S(1)} %bitcast.122), kind=kLoop, calls=%fused_computation.5 | loop fusion | flops 12576768 | bytes 65536 | tf_op jit(solution)/shard_map/reduce_sum | solution.py:102
  61.2 9.2 %collective-permute-done.2 = bf16[512,1024]{1,0:T(8,128)(2,1)S(1)} collective-permute-done((bf16[512,1024]{1,0:T(8,128)(2,1)S(1)}, bf16[512,1024]{1,0:T(8,128)(2,1)S(1)}, u32[]{:S(2)}, u32[]{:S(2)}) %collective-permute-start.2) | collective-permute-done | bytes 1048608 | tf_op jit(solution)/shard_map/ppermute | solution.py:112
  71.2 0.3 constant_dynamic-slice_fusion.3
  71.5 2.5 %concatenate.14 = bf16[513,4096]{1,0:T(8,128)(2,1)} pad(bf16[512,4096]{1,0:T(8,128)(2,1)S(1)} %constant_dynamic-slice_fusion.3, bf16[]{:T(256)} %constant.92.clone.1), padding=0_1x0_0 | pad | bytes 8396802 | tf_op jit(solution)/shard_map/concatenate | solution.py:118
  73.9 25.0 %gather_fusion = bf16[1536,4096]{1,0:T(8,128)(2,1)} fusion(bf16[513,4096]{1,0:T(8,128)(2,1)} %concatenate.14, s32[2048]{0:T(1024)S(1)} %pad_clamp_fusion), kind=kCustom, calls=%fused_computation | custom fusion | bytes 25171968 | tf_op jit(solution)/shard_map/gather | solution.py:119
  99.0 21.3 %fusion.11 = bf16[1,4,384,1024]{3,2,1,0:T(8,128)(2,1)S(1)} fusion(bf16[4,384,4096]{2,1,0:T(8,128)(2,1)} %bitcast.99, bf16[4,4096,1024]{2,1,0:T(8,128)(2,1)} %param.15), kind=kOutput, calls=%fused_computation.15 | convolution fusion | flops 12892766208 | bytes 49283072 | tf_op jit(solution)/shard_map/ecf,efg->ecg/dot_general | solution.py:120
  120.3 3.8 %copy.104 = bf16[1,4,384,1024]{2,1,0,3:T(4,128)(2,1)} copy(bf16[1,4,384,1024]{3,2,1,0:T(8,128)(2,1)S(1)} %fusion.11) | data formatting | bytes 6291456 | tf_op jit(solution)/shard_map/broadcast_in_dim | solution.py:121
  124.1 4.1 %all-to-all-start = ((bf16[1,4,384,1024]{2,1,0,3:T(4,128)(2,1)}), bf16[1,4,384,1024]{2,1,0,3:T(4,128)(2,1)S(1)}, u32[]{:S(2)}, u32[]{:S(2)}) async-start(bf16[1,4,384,1024]{2,1,0,3:T(4,128)(2,1)} %copy.104), calls=%async_computation | async-start | bytes 6291456 | tf_op jit(solution)/shard_map/all_to_all | solution.py:122
  128.2 0.5 fusion.59
  131.9 0.2 reduce-window.17
  133.4 0.6 dynamic_slice.31
  134.7 0.6 add_reduce_fusion
  136.8 0.6 dynamic_slice.34
  138.1 26.6 %all-to-all-done = bf16[1,4,384,1024]{2,1,0,3:T(4,128)(2,1)S(1)} async-done(((bf16[1,4,384,1024]{2,1,0,3:T(4,128)(2,1)}), bf16[1,4,384,1024]{2,1,0,3:T(4,128)(2,1)S(1)}, u32[]{:S(2)}, u32[]{:S(2)}) %all-to-all-start) | async-done | bytes 3145760 | tf_op jit(solution)/shard_map/all_to_all | solution.py:122
  164.8 0.6 copy.105
  165.3 3.8 %fusion.8 = bf16[512,256]{0,1:T(8,128)(2,1)S(1)} fusion(f32[512,16]{0,1:T(8,128)S(1)} %select_reduce_fusion.1, bf16[16,384,256]{1,2,0:T(8,128)(2,1)S(1)} %bitcast.101, s32[16,512]{1,0:T(8,128)S(1)} %convolution_convert_fusion.4, pred[16,512]{1,0:T(8,128)(4,1)S(1)} %bitcast.123), kind=kOutput, calls=%fused_computation.11 | convolution fusion | flops 1620967424 | bytes 3481600 | tf_op jit(solution)/shard_map/ect,ecg->teg/dot_general | solution.py:124
  169.1 0.8 copy.106
  (78 shorter events, 2.8 us)
Async XLA Ops:
  0.6 3.3 %slice-start.3 = ((bf16[512,1024]{1,0:T(8,128)(2,1)}), bf16[384,1024]{1,0:T(8,128)(2,1)S(1)}, s32[]{:S(2)}) async-start(bf16[512,1024]{1,0:T(8,128)(2,1)} %param.9), calls=%async_computation.4 | async-start | bytes 1572864 | tf_op jit(solution)/shard_map/slice | solution.py:76
  4.4 2.5 %slice-start.4 = ((bf16[512,1024]{1,0:T(8,128)(2,1)}), bf16[256,1024]{1,0:T(8,128)(2,1)S(1)}, s32[]{:S(2)}) async-start(bf16[512,1024]{1,0:T(8,128)(2,1)} %param.9), calls=%async_computation.5 | async-start | bytes 1048576 | tf_op jit(solution)/shard_map/slice | solution.py:76
  7.6 1.2 copy-start
  8.3 1.9 %slice-start = ((bf16[512,1024]{1,0:T(8,128)(2,1)}), bf16[384,1024]{1,0:T(8,128)(2,1)S(1)}, s32[]{:S(2)}) async-start(bf16[512,1024]{1,0:T(8,128)(2,1)} %param.10), calls=%async_computation.1 | async-start | bytes 1572864 | tf_op jit(solution)/shard_map/slice | solution.py:77
  11.3 4.3 %slice-start.1 = ((bf16[512,1024]{1,0:T(8,128)(2,1)}), bf16[256,1024]{1,0:T(8,128)(2,1)S(1)}, s32[]{:S(2)}) async-start(bf16[512,1024]{1,0:T(8,128)(2,1)} %param.10), calls=%async_computation.2 | async-start | bytes 1048576 | tf_op jit(solution)/shard_map/slice | solution.py:77
  15.7 2.4 %copy-start.10 = (bf16[128,1024]{1,0:T(8,128)(2,1)S(1)}, bf16[128,1024]{1,0:T(8,128)(2,1)}, u32[]{:S(2)}) copy-start(bf16[128,1024]{1,0:T(8,128)(2,1)} %get-tuple-element.9) | copy-start | bytes 786436
  15.9 2.4 %slice-start.5 = ((bf16[512,1024]{1,0:T(8,128)(2,1)}), bf16[128,1024]{1,0:T(8,128)(2,1)S(1)}, s32[]{:S(2)}) async-start(bf16[512,1024]{1,0:T(8,128)(2,1)} %param.9), calls=%async_computation.6 | async-start | bytes 524288 | tf_op jit(solution)/shard_map/slice | solution.py:76
  15.9 3.0 %slice-start.2 = ((bf16[512,1024]{1,0:T(8,128)(2,1)}), bf16[128,1024]{1,0:T(8,128)(2,1)S(1)}, s32[]{:S(2)}) async-start(bf16[512,1024]{1,0:T(8,128)(2,1)} %param.10), calls=%async_computation.3 | async-start | bytes 524288 | tf_op jit(solution)/shard_map/slice | solution.py:77
  18.0 8.2 %copy-start.1 = (bf16[128,1024]{1,0:T(8,128)(2,1)}, bf16[128,1024]{1,0:T(8,128)(2,1)S(1)}, u32[]{:S(2)}) copy-start(bf16[128,1024]{1,0:T(8,128)(2,1)S(1)} %copy.101) | copy-start | bytes 786436
  18.3 3.3 %copy-start.7 = (bf16[512,1024]{1,0:T(8,128)(2,1)S(1)}, bf16[512,1024]{1,0:T(8,128)(2,1)}, u32[]{:S(2)}) copy-start(bf16[512,1024]{1,0:T(8,128)(2,1)} %param.9) | copy-start | bytes 3145732
  20.1 3.9 %copy-start.9 = (bf16[512,1024]{0,1:T(8,128)(2,1)S(1)}, bf16[512,1024]{0,1:T(8,128)(2,1)}, u32[]{:S(2)}) copy-start(bf16[512,1024]{0,1:T(8,128)(2,1)} %copy.115) | copy-start | bytes 3145732
  21.3 5.0 %copy-start.3 = (bf16[128,1024]{1,0:T(8,128)(2,1)}, bf16[128,1024]{1,0:T(8,128)(2,1)S(1)}, u32[]{:S(2)}) copy-start(bf16[128,1024]{1,0:T(8,128)(2,1)S(1)} %copy.100) | copy-start | bytes 786436
  23.9 18.1 %copy-start.11 = (s32[512,8]{0,1:T(8,128)S(1)}, s32[512,8]{0,1:T(8,128)}, u32[]{:S(2)}) copy-start(s32[512,8]{0,1:T(8,128)} %param.13) | copy-start | bytes 49156
  26.3 0.7 copy-start.5
  27.0 1.0 copy-start.8
  27.0 14.9 %collective-permute-start = (bf16[512,1024]{1,0:T(8,128)(2,1)S(1)}, bf16[512,1024]{1,0:T(8,128)(2,1)S(1)}, u32[]{:S(2)}, u32[]{:S(2)}) collective-permute-start(bf16[512,1024]{1,0:T(8,128)(2,1)S(1)} %pad_maximum_fusion), channel_id=1, source_target_pairs={{0,1},{1,2},{2,3},{3,0},{4,5},{5,6},{6,7},{7,4},{8,9},{9,10},{10,1... | collective-permute-start | bytes 3145736 | tf_op jit(solution)/shard_map/ppermute | solution.py:112
  42.0 14.2 %collective-permute-start.1 = (bf16[512,1024]{1,0:T(8,128)(2,1)S(1)}, bf16[512,1024]{1,0:T(8,128)(2,1)S(1)}, u32[]{:S(2)}, u32[]{:S(2)}) collective-permute-start(bf16[512,1024]{1,0:T(8,128)(2,1)S(1)} %collective-permute-done), channel_id=1, source_target_pairs={{0,1},{1,2},{2,3},{3,0},{4,5},{5,6},{6,7},{7,4},{8,9},{9,10},{10,1... | collective-permute-start | bytes 3145736 | tf_op jit(solution)/shard_map/ppermute | solution.py:112
  56.2 14.2 %collective-permute-start.2 = (bf16[512,1024]{1,0:T(8,128)(2,1)S(1)}, bf16[512,1024]{1,0:T(8,128)(2,1)S(1)}, u32[]{:S(2)}, u32[]{:S(2)}) collective-permute-start(bf16[512,1024]{1,0:T(8,128)(2,1)S(1)} %collective-permute-done.1), channel_id=1, source_target_pairs={{0,1},{1,2},{2,3},{3,0},{4,5},{5,6},{6,7},{7,4},{8,9},{9,10},{10,1... | collective-permute-start | bytes 3145736 | tf_op jit(solution)/shard_map/ppermute | solution.py:112
  61.2 9.5 %copy-start.2 = (bf16[128,1024]{1,0:T(8,128)(2,1)S(1)}, bf16[128,1024]{1,0:T(8,128)(2,1)}, u32[]{:S(2)}) copy-start(bf16[128,1024]{1,0:T(8,128)(2,1)} %copy-done.1) | copy-start | bytes 786436
  61.2 9.5 %copy-start.4 = (bf16[128,1024]{1,0:T(8,128)(2,1)S(1)}, bf16[128,1024]{1,0:T(8,128)(2,1)}, u32[]{:S(2)}) copy-start(bf16[128,1024]{1,0:T(8,128)(2,1)} %copy-done.3) | copy-start | bytes 786436
  61.2 9.5 %copy-start.6 = (bf16[128,1024]{1,0:T(8,128)(2,1)S(1)}, bf16[128,1024]{1,0:T(8,128)(2,1)}, u32[]{:S(2)}) copy-start(bf16[128,1024]{1,0:T(8,128)(2,1)} %copy-done.5) | copy-start | bytes 786436
  124.1 4.1 %copy-start.13 = (s32[8,2]{0,1:T(2,128)S(1)}, s32[8,2]{0,1:T(2,128)}, u32[]{:S(2)}) copy-start(s32[8,2]{0,1:T(2,128)} %param.12) | copy-start | bytes 196
  124.1 14.0 %copy-start.12 = (f32[512,8]{0,1:T(8,128)S(1)}, f32[512,8]{0,1:T(8,128)}, u32[]{:S(2)}) copy-start(f32[512,8]{0,1:T(8,128)} %param.14) | copy-start | bytes 49156
  124.1 40.7 %all-to-all-start = ((bf16[1,4,384,1024]{2,1,0,3:T(4,128)(2,1)}), bf16[1,4,384,1024]{2,1,0,3:T(4,128)(2,1)S(1)}, u32[]{:S(2)}, u32[]{:S(2)}) async-start(bf16[1,4,384,1024]{2,1,0,3:T(4,128)(2,1)} %copy.104), calls=%async_computation | async-start | bytes 6291456 | tf_op jit(solution)/shard_map/all_to_all | solution.py:122
